TPU v7x, 256 devices: a whole 4x4x8 slice. The times are simulated.
256 devices in a mesh: expert: 8 (over x, core), replica: 32 (over y, z).
Axes of the slice: x: 4, y: 4, z: 8, core: 2. Of those that a mesh axis runs over, the one named last changes fastest.
Arguments:
- tokens: bfloat16 [1536, 4096], P(('expert', 'replica')), may hold values from -6 to 6
- out_grad: bfloat16 [1536, 4096], P(('expert', 'replica')), may hold values from -2.5 to 2.5
- expert_ids: int32 [1536, 2], P(('expert', 'replica')), may hold values from 0 to 7, all different within a row; in each aligned block of 6 rows (0 to 5, 6 to 11, ...) at most 2 rows name the same one
- gates: float32 [1536, 2], P(('expert', 'replica')), may hold values from 0.1 to 1
- w_gate: bfloat16 [8, 7168, 4096], P('expert', 'replica'), may hold values from -0.09375 to 0.09375
- w_up: bfloat16 [8, 7168, 4096], P('expert', 'replica'), may hold values from -0.09375 to 0.09375
- w_down: bfloat16 [8, 7168, 4096], P('expert', 'replica'), may hold values from -0.0625 to 0.0625
Outputs:
- gate_grad: float32 [1536, 2], P(('expert', 'replica'))
- input_grad: bfloat16 [1536, 4096], P(('expert', 'replica'))
- grad_gate: bfloat16 [8, 7168, 4096], P('expert', 'replica')
- grad_up: bfloat16 [8, 7168, 4096], P('expert', 'replica')
- grad_down: bfloat16 [8, 7168, 4096], P('expert', 'replica')
Inputs may be any that keep to these rules, and one draw needn't show every extreme that they name: `expert_ids`: each row names 2 different experts; among the rows of one device no expert is named more than 2 times.
All inputs are finite; a program needn't handle non-finite values.
Results may differ from a plain program's by a relative error of at most 0.02.
Values may be sent and summed in bfloat16 or wider, within the bound.
No kernel may reach another device: no remote copies, remote signals or barrier semaphores. Data moves between devices by JAX's collectives and lax.ppermute only.
A program may use at most 128 MiB of HBM per device.

v0:
```python
import jax
import jax.numpy as jnp
from jax import lax
from jax.sharding import Mesh
from jax.sharding import PartitionSpec as P

REPLICA = ("replica_0", "replica_1")
EXPERT_REPLICA = ("expert", "replica_0", "replica_1")


def split_up(value, dim, peers):
    shape = value.shape
    tiles = value.reshape(*shape[:dim], peers, shape[dim] // peers, *shape[dim + 1 :])
    return jnp.moveaxis(tiles, dim, 0)


def sum_at_owner(value, axis, dim):
    peers = lax.axis_size(axis)
    tiles = lax.all_to_all(split_up(value, dim, peers), axis, 0, 0, tiled=True)
    return jnp.sum(tiles, axis=0)


def own_rows(terms, axes):
    running = terms.astype(jnp.bfloat16)
    for axis in axes:
        running = lax.psum_scatter(running, axis, scatter_dimension=0, tiled=True)
    return running.astype(jnp.float32)


def on_device(tokens, out_grad, expert_ids, gates, w_gate, w_up, w_down):
    token_count = tokens.shape[0]
    fan_out = expert_ids.shape[1]
    model_width = tokens.shape[1]
    owners = lax.axis_size("expert")
    capacity = max(2, 4 * token_count * fan_out // (3 * owners))
    slot_count = owners * capacity
    flat_ids = expert_ids.reshape(-1)
    sequence_pos = jnp.arange(token_count * fan_out, dtype=jnp.int32)
    earlier = sequence_pos[None, :] < sequence_pos[:, None]
    same_expert = flat_ids[:, None] == flat_ids[None, :]
    slot_rank = jnp.sum(jnp.logical_and(same_expert, earlier), axis=1)
    target = flat_ids * capacity + slot_rank
    token_hot = (target[:, None] == jnp.arange(slot_count, dtype=jnp.int32)[None, :]).astype(
        jnp.float32
    )
    token_hot = token_hot.reshape(token_count, fan_out, slot_count)
    dispatch = jnp.sum(token_hot, axis=1).astype(jnp.bfloat16)
    slot_gate = jnp.sum(token_hot * gates[:, :, None], axis=(0, 1)).reshape(owners, capacity)
    leading = (((0,), (0,)), ((), ()))
    contract = (((1,), (1,)), ((), ()))
    send_inputs = (
        lax.dot_general(dispatch, tokens, leading, preferred_element_type=jnp.float32)
        .astype(jnp.bfloat16)
        .reshape(owners, capacity, model_width)
    )
    send_grads = (
        lax.dot_general(dispatch, out_grad, leading, preferred_element_type=jnp.float32)
        .astype(jnp.bfloat16)
        .reshape(owners, capacity, model_width)
    )
    gate_weight = w_gate[0]
    up_weight = w_up[0]
    down_weight = w_down[0]
    owned = (
        lax.all_to_all(send_inputs, "expert", split_axis=0, concat_axis=0, tiled=True),
        lax.all_to_all(send_grads, "expert", split_axis=0, concat_axis=0, tiled=True),
        lax.all_to_all(
            slot_gate.astype(jnp.bfloat16), "expert", split_axis=0, concat_axis=0, tiled=True
        ).astype(slot_gate.dtype),
    )
    column_inputs, column_grads, column_gates = (
        lax.all_gather(owned[0], REPLICA, axis=0, tiled=True),
        lax.all_gather(owned[1], REPLICA, axis=0, tiled=True),
        lax.all_gather(owned[2].astype(jnp.bfloat16), REPLICA, axis=0, tiled=True).astype(
            jnp.float32
        ),
    )
    gathered = column_inputs.reshape(-1, model_width)
    gate_pre = lax.dot_general(gathered, gate_weight, contract, preferred_element_type=jnp.float32)
    up_pre = lax.dot_general(gathered, up_weight, contract, preferred_element_type=jnp.float32)
    sigmoid_gate = jax.nn.sigmoid(gate_pre)
    active = gate_pre * sigmoid_gate
    hidden = (active * up_pre).astype(jnp.bfloat16)
    gathered_grad = column_grads.reshape(-1, model_width)
    row_gates = column_gates.reshape(-1)
    full_out = jnp.dot(hidden, down_weight, preferred_element_type=jnp.float32)
    partial_value = jnp.sum(gathered_grad * full_out, axis=1)
    summed_products = sum_at_owner(partial_value, REPLICA, 0)
    returned = lax.all_to_all(
        summed_products.reshape(owners, capacity), "expert", split_axis=0, concat_axis=0, tiled=True
    )
    gate_grad = jnp.sum(token_hot * returned.reshape(-1)[None, None, :], axis=2)
    scaled = (row_gates[:, None] * gathered_grad).astype(jnp.bfloat16)
    hidden_grad = lax.dot_general(scaled, down_weight, contract, preferred_element_type=jnp.float32)
    gate_pre_grad = (
        hidden_grad * up_pre * sigmoid_gate * (1.0 + gate_pre * (1.0 - sigmoid_gate))
    ).astype(jnp.bfloat16)
    up_pre_grad = (hidden_grad * active).astype(jnp.bfloat16)
    grad_down = lax.dot_general(hidden, scaled, leading, preferred_element_type=jnp.float32).astype(
        jnp.bfloat16
    )
    grad_gate = lax.dot_general(
        gate_pre_grad, gathered, leading, preferred_element_type=jnp.float32
    ).astype(jnp.bfloat16)
    grad_up = lax.dot_general(
        up_pre_grad, gathered, leading, preferred_element_type=jnp.float32
    ).astype(jnp.bfloat16)
    slot_grad = own_rows(
        jnp.dot(gate_pre_grad, gate_weight, preferred_element_type=jnp.float32)
        + jnp.dot(up_pre_grad, up_weight, preferred_element_type=jnp.float32),
        REPLICA,
    ).astype(jnp.bfloat16)
    slot_back = lax.all_to_all(
        slot_grad.reshape(owners, capacity, model_width),
        "expert",
        split_axis=0,
        concat_axis=0,
        tiled=True,
    )
    slot_back = slot_back.reshape(slot_count, model_width)
    input_grad = jnp.dot(dispatch, slot_back, preferred_element_type=jnp.float32).astype(
        jnp.bfloat16
    )
    return (gate_grad, input_grad, grad_gate[None], grad_up[None], grad_down[None])


def solution(mesh):
    torus = Mesh(
        mesh.devices.reshape(mesh.shape["expert"], 4, 8), ("expert", "replica_0", "replica_1")
    )
    in_specs = (
        P(EXPERT_REPLICA, None),
        P(EXPERT_REPLICA, None),
        P(EXPERT_REPLICA, None),
        P(EXPERT_REPLICA, None),
        P("expert", REPLICA, None),
        P("expert", REPLICA, None),
        P("expert", REPLICA, None),
    )
    out_specs = (
        P(EXPERT_REPLICA, None),
        P(EXPERT_REPLICA, None),
        P("expert", REPLICA, None),
        P("expert", REPLICA, None),
        P("expert", REPLICA, None),
    )
    return jax.shard_map(
        on_device, mesh=torus, in_specs=in_specs, out_specs=out_specs, check_vma=False
    )
```

profile of v0, /device:TPU:1, one launch (start us, length us, event | category | flops | bytes accessed | tf_op | source)
XLA Modules:
  0.0 404.9 jit_solution(4118786558378128443)
XLA Ops:
  9.8 11.5 %all_to_all.42 = bf16[8,2,4096]{2,1,0:T(2,128)(2,1)} all-to-all(bf16[8,2,4096]{2,1,0:T(2,128)(2,1)S(1)} %reshape.81), channel_id=1, replica_groups=mesh['expert'=8,'replica_0'=4,'replica_1'=8] {'expert'}, dimensions={0} | all-to-all | bytes 262144 | tf_op jit(solution)/shard_map/all_to_all | solution.py:65
  22.5 9.2 %all_to_all.43 = bf16[8,2,4096]{2,1,0:T(2,128)(2,1)} all-to-all(bf16[8,2,4096]{2,1,0:T(2,128)(2,1)S(1)} %reshape.80), channel_id=1, replica_groups=mesh['expert'=8,'replica_0'=4,'replica_1'=8] {'expert'}, dimensions={0} | all-to-all | bytes 262144 | tf_op jit(solution)/shard_map/all_to_all | solution.py:66
  31.7 68.7 %all-gather.6.cloned.1.call-done = bf16[256,2,4096]{2,1,0:T(2,128)(2,1)} async-done(((bf16[8,2,4096]{2,1,0:T(2,128)(2,1)}), bf16[256,2,4096]{2,1,0:T(2,128)(2,1)}) %all-gather.6.cloned.1.call-update) | async-done | bytes 4194320 | tf_op jit(solution)/shard_map/all_gather | solution.py:72
  100.4 7.2 %reshape.82 = bf16[512,4096]{1,0:T(8,128)(2,1)} reshape(bf16[256,2,4096]{2,1,0:T(2,128)(2,1)} %all-gather.6.cloned.1.call-done) | data formatting | bytes 8388608 | tf_op jit(solution)/shard_map/reshape | solution.py:78
  107.6 4.3 %fusion.12 = f32[512,224]{0,1:T(8,128)S(1)} fusion(bf16[512,4096]{1,0:T(8,128)(2,1)} %reshape.82, bf16[1,224,4096]{2,1,0:T(8,128)(2,1)} %param.11), kind=kOutput, calls=%fused_computation.22 | convolution fusion | flops 939524096 | bytes 6488064 | tf_op jit(solution)/shard_map/dot_general | solution.py:79
  112.0 2.3 multiply_convert_fusion.5
  114.3 67.3 %all-gather.4.cloned.1.call-done = bf16[256,2,4096]{2,1,0:T(2,128)(2,1)} async-done(((bf16[8,2,4096]{2,1,0:T(2,128)(2,1)}), bf16[256,2,4096]{2,1,0:T(2,128)(2,1)}) %all-gather.4.cloned.1.call-update) | async-done | bytes 4194320 | tf_op jit(solution)/shard_map/all_gather | solution.py:73
  181.6 7.6 %reshape.85 = f32[512,4096]{1,0:T(8,128)} reshape(bf16[256,2,4096]{2,1,0:T(2,128)(2,1)} %all-gather.4.cloned.1.call-done) | data formatting | bytes 12582912 | tf_op jit(solution)/shard_map/convert_element_type | solution.py:87
  189.2 5.3 %multiply_reduce_fusion = f32[512]{0:T(512)S(1)} fusion(f32[512,4096]{1,0:T(8,128)} %reshape.85, bf16[512,224]{0,1:T(8,128)(2,1)S(1)} %get-tuple-element.14, bf16[1,224,4096]{2,1,0:T(8,128)(2,1)} %param.13), kind=kOutput, calls=%fused_computation.3 | convolution fusion | flops 943717888 | bytes 10455040 | tf_op jit(solution)/shard_map/dot_general | solution.py:86
  194.6 14.5 %all_to_all.44 = f32[32,1,16]{2,1,0:T(1,128)S(1)} all-to-all(f32[32,1,16]{2,1,0:T(1,128)S(1)} %bitcast.46), channel_id=1, replica_groups=mesh['expert'=8,'replica_0'=4,'replica_1'=8] {'replica_0','replica_1'}, dimensions={0} | all-to-all | bytes 4096 | tf_op jit(solution)/shard_map/all_to_all | solution.py:19
  209.8 8.9 %all-to-all-start.3 = ((f32[8,1,2]{2,1,0:T(1,128)}), f32[8,1,2]{2,1,0:T(1,128)S(1)}, u32[]{:S(2)}, u32[]{:S(2)}) async-start(f32[8,1,2]{2,1,0:T(1,128)} %bitcast.4), calls=%async_computation.3 | async-start | bytes 8192 | tf_op jit(solution)/shard_map/all_to_all | solution.py:89
  218.8 4.4 %all-to-all-done.3 = f32[8,1,2]{2,1,0:T(1,128)S(1)} async-done(((f32[8,1,2]{2,1,0:T(1,128)}), f32[8,1,2]{2,1,0:T(1,128)S(1)}, u32[]{:S(2)}, u32[]{:S(2)}) %all-to-all-start.3) | async-done | bytes 96 | tf_op jit(solution)/shard_map/all_to_all | solution.py:89
  224.8 7.6 %all_to_all.45 = bf16[8,1,2]{2,1,0:T(2,128)(2,1)S(1)} all-to-all(bf16[8,1,2]{2,1,0:T(2,128)(2,1)S(1)} %convert_element_type.102), channel_id=1, replica_groups=mesh['expert'=8,'replica_0'=4,'replica_1'=8] {'expert'}, dimensions={0} | all-to-all | bytes 64 | tf_op jit(solution)/shard_map/all_to_all | solution.py:67
  232.4 31.3 %all-gather = bf16[256,1,2]{2,1,0:T(2,128)(2,1)S(1)} all-gather(bf16[8,1,2]{2,1,0:T(2,128)(2,1)S(1)} %all_to_all.45), channel_id=2, replica_groups=mesh['expert'=8,'replica_0'=4,'replica_1'=8] {'replica_0','replica_1'}, dimensions={0}, use_global_device_ids=true | all-gather | bytes 1056 | tf_op jit(solution)/shard_map/all_gather | solution.py:74
  263.8 10.4 %multiply_convert_fusion.1 = bf16[256,2,4096]{2,1,0:T(2,128)(2,1)} fusion(f32[256,2]{1,0:T(8,128)S(1)} %bitcast.45, bf16[256,2,4096]{2,1,0:T(2,128)(2,1)} %all-gather.4.cloned.1.call-done), kind=kLoop, calls=%fused_computation.2 | loop fusion | flops 6291456 | bytes 8390656 | tf_op jit(solution)/shard_map/convert_element_type | solution.py:93
  274.2 7.2 %convert_element_type.91 = bf16[512,4096]{1,0:T(8,128)(2,1)} reshape(bf16[256,2,4096]{2,1,0:T(2,128)(2,1)} %multiply_convert_fusion.1) | data formatting | bytes 8388608 | tf_op jit(solution)/shard_map/convert_element_type | solution.py:93
  281.4 4.4 %multiply_convert_fusion.3 = (bf16[512,224]{0,1:T(8,128)(2,1)S(1)}, bf16[512,224]{0,1:T(8,128)(2,1)S(1)}) fusion(f32[512,224]{0,1:T(8,128)S(1)} %fusion.12, f32[512,224]{0,1:T(8,128)} %get-tuple-element.15, bf16[512,4096]{1,0:T(8,128)(2,1)} %convert_element_type.91, bf16[1,224,4096]{2,1,0:T(8,128)(2,1)} %param.13), kind=kOutput, calls=%fused_computation.24 | convolution fusion | flops 941015040 | bytes 7405568 | tf_op jit(solution)/shard_map/dot_general | solution.py:94
  287.1 3.3 add_convert_fusion
  290.7 53.7 %reduce-scatter.3.cloned.1.call-done = bf16[128,4096]{1,0:T(8,128)(2,1)} async-done(((bf16[512,4096]{1,0:T(8,128)(2,1)}), bf16[128,4096]{1,0:T(8,128)(2,1)}) %reduce-scatter.3.cloned.1.call-update) | async-done | bytes 1048592 | tf_op jit(solution)/shard_map/reduce_scatter | solution.py:26
  345.6 4.5 %fusion.1 = bf16[1,224,4096]{2,1,0:T(8,128)(2,1)} fusion(bf16[512,224]{0,1:T(8,128)(2,1)S(1)} %get-tuple-element.12, bf16[512,4096]{1,0:T(8,128)(2,1)} %reshape.82), kind=kOutput, calls=%fused_computation.8 | convolution fusion | flops 940441600 | bytes 6258688 | tf_op jit(solution)/shard_map/dot_general | solution.py:105
  350.2 5.8 %fusion.2 = bf16[1,224,4096]{2,1,0:T(8,128)(2,1)} fusion(bf16[512,224]{0,1:T(8,128)(2,1)S(1)} %get-tuple-element.14, f32[512,4096]{1,0:T(8,128)} %reshape.85, f32[512]{0:T(512)S(1)} %mul.80), kind=kOutput, calls=%fused_computation.9 | convolution fusion | flops 944635904 | bytes 10455040 | tf_op jit(solution)/shard_map/dot_general | solution.py:99
  356.0 24.6 %reduce-scatter.5.cloned.1.call-done = bf16[16,4096]{1,0:T(8,128)(2,1)} async-done(((bf16[128,4096]{1,0:T(8,128)(2,1)}), bf16[16,4096]{1,0:T(8,128)(2,1)}) %reduce-scatter.5.cloned.1.call-update) | async-done | bytes 131088 | tf_op jit(solution)/shard_map/reduce_scatter | solution.py:26
  382.3 10.0 %all-to-all-start.5 = ((bf16[8,2,4096]{2,1,0:T(2,128)(2,1)}), bf16[8,2,4096]{2,1,0:T(2,128)(2,1)S(1)}, u32[]{:S(2)}, u32[]{:S(2)}) async-start(bf16[8,2,4096]{2,1,0:T(2,128)(2,1)} %reshape.83), calls=%async_computation.7 | async-start | bytes 262144 | tf_op jit(solution)/shard_map/all_to_all | solution.py:113
  392.3 4.5 %fusion = bf16[1,224,4096]{2,1,0:T(8,128)(2,1)} fusion(bf16[512,224]{0,1:T(8,128)(2,1)S(1)} %get-tuple-element.13, bf16[512,4096]{1,0:T(8,128)(2,1)} %reshape.82), kind=kOutput, calls=%fused_computation.7 | convolution fusion | flops 940441600 | bytes 6258688 | tf_op jit(solution)/shard_map/dot_general | solution.py:102
  (44 shorter events, 12.3 us)
Async XLA Ops:
  7.2 104.8 %copy-start = (bf16[1,224,4096]{2,1,0:T(8,128)(2,1)S(1)}, bf16[1,224,4096]{2,1,0:T(8,128)(2,1)}, u32[]{:S(2)}) copy-start(bf16[1,224,4096]{2,1,0:T(8,128)(2,1)} %param.12) | copy-start | bytes 5505028
  7.2 93.2 %all-gather.6.cloned.1.call-start = ((), (), s32[]{:S(2)}) async-start(), calls=%async_computation.9 | async-start | bytes 4325376 | tf_op jit(solution)/shard_map/all_gather | solution.py:72
  21.3 160.3 %all-gather.4.cloned.1.call-start = ((), (), s32[]{:S(2)}) async-start(), calls=%async_computation.8 | async-start | bytes 4325376 | tf_op jit(solution)/shard_map/all_gather | solution.py:73
  107.6 4.4 %copy-start.1 = (bf16[512,4096]{1,0:T(8,128)(2,1)S(1)}, bf16[512,4096]{1,0:T(8,128)(2,1)}, u32[]{:S(2)}) copy-start(bf16[512,4096]{1,0:T(8,128)(2,1)} %reshape.82) | copy-start | bytes 12582916
  189.2 29.6 %copy-start.3 = (f32[6,2]{0,1:T(2,128)S(1)}, f32[6,2]{0,1:T(2,128)}, u32[]{:S(2)}) copy-start(f32[6,2]{0,1:T(2,128)} %param.10) | copy-start | bytes 148
  209.8 13.5 %all-to-all-start.3 = ((f32[8,1,2]{2,1,0:T(1,128)}), f32[8,1,2]{2,1,0:T(1,128)S(1)}, u32[]{:S(2)}, u32[]{:S(2)}) async-start(f32[8,1,2]{2,1,0:T(1,128)} %bitcast.4), calls=%async_computation.3 | async-start | bytes 8192 | tf_op jit(solution)/shard_map/all_to_all | solution.py:89
  218.7 125.7 %reduce-scatter.3.cloned.1.call-start = ((), (), s32[]{:S(2)}) async-start(), calls=%async_computation.10 | async-start | bytes 5242880 | tf_op jit(solution)/shard_map/reduce_scatter | solution.py:26
  281.4 4.4 %copy-start.2 = (bf16[1,224,4096]{2,1,0:T(8,128)(2,1)S(1)}, bf16[1,224,4096]{2,1,0:T(8,128)(2,1)}, u32[]{:S(2)}) copy-start(bf16[1,224,4096]{2,1,0:T(8,128)(2,1)} %param.11) | copy-start | bytes 5505028
  290.5 90.2 %reduce-scatter.5.cloned.1.call-start = ((), (), s32[]{:S(2)}) async-start(), calls=%async_computation.11 | async-start | bytes 1179648 | tf_op jit(solution)/shard_map/reduce_scatter | solution.py:26
  382.3 15.3 %all-to-all-start.5 = ((bf16[8,2,4096]{2,1,0:T(2,128)(2,1)}), bf16[8,2,4096]{2,1,0:T(2,128)(2,1)S(1)}, u32[]{:S(2)}, u32[]{:S(2)}) async-start(bf16[8,2,4096]{2,1,0:T(2,128)(2,1)} %reshape.83), calls=%async_computation.7 | async-start | bytes 262144 | tf_op jit(solution)/shard_map/all_to_all | solution.py:113
Sparse Core Ops, SparseCore 0:
  21.4 78.9 all-gather.5
  103.0 78.5 all-gather.3
  290.6 53.7 reduce-scatter.2
  346.8 33.7 reduce-scatter.4
where the time goes:
time: 406 us; the launch traced here: 405 us
  waiting for transfers between devices  220 us (54%)
  blocking collectives  74 us (18%)
  matrix products  38.8 us (10%)
  local copies, waits for them, and re-layouts  27.3 us (7%)
  starting transfers between devices  19.3 us (5%)
  between operations  13.9 us (3%)
  other arithmetic  12 us (3%)
    reduce_scatter x2, waiting for transfers between devices, own_rows(): running = lax.psum_scatter(running, axis, scatter_dimension=0, tiled=True)  78.3 us
    all_gather x1, waiting for transfers between devices, on_device(): lax.all_gather(owned[0], REPLICA, axis=0, tiled=True)  68.7 us
    all_gather x1, waiting for transfers between devices, on_device(): lax.all_gather(owned[1], REPLICA, axis=0, tiled=True)  67.3 us
    all_gather x1, blocking collectives, on_device(): lax.all_gather(owned[2].astype(jnp.bfloat16), REPLICA, axis=0, tiled=True)  31.3 us
    all_to_all x1, blocking collectives, sum_at_owner(): tiles = lax.all_to_all(split_up(value, dim, peers), axis, 0, 0, tiled=True)  14.5 us
    all_to_all x1, blocking collectives, on_device(): lax.all_to_all(send_inputs, 'expert', split_axis=0, concat_axis=0, tiled=...  11.5 us
    convert_element_type x1, other arithmetic, on_device(): scaled = (row_gates[:, None] * gathered_grad).astype(jnp.bfloat16)  10.4 us
    all_to_all x1, starting transfers between devices, on_device(): lax.all_to_all(slot_grad.reshape(owners, capacity, model_width), 'expert'...  10 us
  transfers between devices with their start and end apart: 6, of which 6 were waited for; matrix products, arithmetic and copies ran while one was open for 8% of the time, Pallas kernels for 0%

commit v1 on v0

v1 whole, which is shorter than its diff:
```python
import jax
import jax.numpy as jnp
from jax import lax
from jax.sharding import Mesh
from jax.sharding import PartitionSpec as P

REPLICA = ("replica_0", "replica_1")
EXPERT_REPLICA = ("expert", "replica_0", "replica_1")
HOME = ("replica_0", "expert")


def on_device(tokens, out_grad, expert_ids, gates, w_gate, w_up, w_down):
    token_count = tokens.shape[0]
    fan_out = expert_ids.shape[1]
    model_width = tokens.shape[1]
    owners = lax.axis_size("expert")
    rows_y = lax.axis_size("replica_0")
    rows_z = lax.axis_size("replica_1")
    capacity = max(2, 4 * token_count * fan_out // (3 * owners))
    slot_count = owners * capacity
    flat_ids = expert_ids.reshape(-1)
    sequence_pos = jnp.arange(token_count * fan_out, dtype=jnp.int32)
    earlier = sequence_pos[None, :] < sequence_pos[:, None]
    same_expert = flat_ids[:, None] == flat_ids[None, :]
    slot_rank = jnp.sum(jnp.logical_and(same_expert, earlier), axis=1)
    target = flat_ids * capacity + slot_rank
    token_hot = (target[:, None] == jnp.arange(slot_count, dtype=jnp.int32)[None, :]).astype(
        jnp.float32
    )
    token_hot = token_hot.reshape(token_count, fan_out, slot_count)
    dispatch = jnp.sum(token_hot, axis=1).astype(jnp.bfloat16)
    slot_gate = jnp.sum(token_hot * gates[:, :, None], axis=(0, 1))
    leading = (((0,), (0,)), ((), ()))
    contract = (((1,), (1,)), ((), ()))
    picked = lax.dot_general(
        dispatch,
        jnp.concatenate([tokens, out_grad], axis=1),
        leading,
        preferred_element_type=jnp.float32,
    )
    scale = jnp.concatenate(
        [
            jnp.ones((slot_count, model_width), jnp.float32),
            jnp.broadcast_to(slot_gate[:, None], (slot_count, model_width)),
        ],
        axis=1,
    )
    send = (picked * scale).astype(jnp.bfloat16)
    gate_weight = w_gate[0]
    up_weight = w_up[0]
    down_weight = w_down[0]
    owned = lax.all_to_all(
        send.reshape(owners, capacity, 2 * model_width), "expert", 0, 0, tiled=True
    ).reshape(slot_count, 2 * model_width)
    column = lax.all_gather(owned, REPLICA, axis=0, tiled=True)
    gathered = column[:, :model_width]
    scaled = column[:, model_width:]
    gate_pre = lax.dot_general(gathered, gate_weight, contract, preferred_element_type=jnp.float32)
    up_pre = lax.dot_general(gathered, up_weight, contract, preferred_element_type=jnp.float32)
    hidden_grad = lax.dot_general(scaled, down_weight, contract, preferred_element_type=jnp.float32)
    sigmoid_gate = jax.nn.sigmoid(gate_pre)
    active = gate_pre * sigmoid_gate
    hidden = (active * up_pre).astype(jnp.bfloat16)
    partial_value = jnp.sum(hidden.astype(jnp.float32) * hidden_grad, axis=1)
    gate_pre_grad = (
        hidden_grad * up_pre * sigmoid_gate * (1.0 + gate_pre * (1.0 - sigmoid_gate))
    ).astype(jnp.bfloat16)
    up_pre_grad = (hidden_grad * active).astype(jnp.bfloat16)

    def by_z(value):
        tiles = value.reshape(rows_y, rows_z, slot_count, value.shape[1])
        return jnp.swapaxes(tiles, 0, 1).reshape(value.shape)

    slot_grad = (
        jnp.dot(by_z(gate_pre_grad), gate_weight, preferred_element_type=jnp.float32)
        + jnp.dot(by_z(up_pre_grad), up_weight, preferred_element_type=jnp.float32)
    ).astype(jnp.bfloat16)
    summed_z = lax.psum_scatter(slot_grad, "replica_1", scatter_dimension=0, tiled=True)
    tiles = lax.all_to_all(
        partial_value.reshape(rows_y * rows_z, slot_count), REPLICA, 0, 0, tiled=True
    )
    returned = lax.all_to_all(
        jnp.sum(tiles, axis=0).reshape(owners, capacity), "expert", 0, 0, tiled=True
    )
    product = jnp.sum(token_hot * returned.reshape(-1)[None, None, :], axis=2)
    gate_grad = product / gates
    grad_down = lax.dot_general(hidden, scaled, leading, preferred_element_type=jnp.float32).astype(
        jnp.bfloat16
    )
    grad_gate = lax.dot_general(
        gate_pre_grad, gathered, leading, preferred_element_type=jnp.float32
    ).astype(jnp.bfloat16)
    grad_up = lax.dot_general(
        up_pre_grad, gathered, leading, preferred_element_type=jnp.float32
    ).astype(jnp.bfloat16)
    slot_back = lax.all_to_all(
        summed_z.reshape(rows_y * owners, capacity, model_width), HOME, 0, 0, tiled=True
    ).reshape(rows_y * slot_count, model_width)
    input_grad = jnp.dot(
        jnp.concatenate([dispatch] * rows_y, axis=1),
        slot_back,
        preferred_element_type=jnp.float32,
    ).astype(jnp.bfloat16)
    return (gate_grad, input_grad, grad_gate[None], grad_up[None], grad_down[None])


def solution(mesh):
    torus = Mesh(
        mesh.devices.reshape(mesh.shape["expert"], 4, 8), ("expert", "replica_0", "replica_1")
    )
    in_specs = (
        P(EXPERT_REPLICA, None),
        P(EXPERT_REPLICA, None),
        P(EXPERT_REPLICA, None),
        P(EXPERT_REPLICA, None),
        P("expert", REPLICA, None),
        P("expert", REPLICA, None),
        P("expert", REPLICA, None),
    )
    out_specs = (
        P(EXPERT_REPLICA, None),
        P(EXPERT_REPLICA, None),
        P("expert", REPLICA, None),
        P("expert", REPLICA, None),
        P("expert", REPLICA, None),
    )
    return jax.shard_map(
        on_device, mesh=torus, in_specs=in_specs, out_specs=out_specs, check_vma=False
    )
```

time: 406 us -> 219 us (0.54)
  waiting for transfers between devices: 220 us -> 134 us
  blocking collectives: 74 us -> 12.1 us
  local copies, waits for them, and re-layouts: 27.3 us -> 9.35 us
  matrix products: 38.8 us -> 27.6 us
  other arithmetic: 12 us -> 1.16 us
    reduce_scatter x2 -> x1, waiting for transfers between devices: 78.3 us -> 30.8 us  [on_device(): lax.psum_scatter(slot_grad, 'replica_1', scatter_dimension=0, tiled=True)]
    all_gather x2 -> x1, waiting for transfers between devices: 136 us -> 98.7 us  [on_device(): column = lax.all_gather(owned, REPLICA, axis=0, tiled=True)]
    all_gather x1 -> x0, blocking collectives: 31.3 us -> none  [on_device(): lax.all_gather(owned[2].astype(jnp.bfloat16), REPLICA, axis=0, tiled=True)]
    all_to_all x4 -> x1, blocking collectives: 42.8 us -> 12.1 us  [on_device(): lax.all_to_all(send.reshape(owners, capacity, 2 * model_width), 'expert',...]
    convert_element_type x3 -> x2, local copies, waits for them, and re-layouts: 14.9 us -> 0.27 us  [the longest x1 0.13 us: on_device(): gate_pre_grad = (hidden_grad * up_pre * sigmoid_gate * (1.0 + gate_pre *...]
    convert_element_type x3 -> x0, other arithmetic: 10.9 us -> none  [the longest x1 10.4 us: on_device(): scaled = (row_gates[:, None] * gathered_grad).astype(jnp.bfloat16)]
    dot_general x6 -> x4, matrix products: 12.8 us -> 6.51 us  [the longest x1 3.23 us: on_device(): jnp.dot(by_z(up_pre_grad), up_weight, preferred_element_type=jnp.float32)]
    reshape x5 -> x4, local copies, waits for them, and re-layouts: 9.12 us -> 3.41 us  [the longest x1 2.22 us: on_device(): summed_z.reshape(rows_y * owners, capacity, model_width)]
  transfers between devices with their start and end apart: 6 -> 5, of which waited for: 6 -> 3; matrix products, arithmetic and copies ran while one was open for 8% -> 8% of each run, Pallas kernels for 0% -> 0%
where the time goes in v1:
time: 219 us; the launch traced here: 218 us
  waiting for transfers between devices  134 us (61%)
  matrix products  27.6 us (13%)
  starting transfers between devices  19.6 us (9%)
  between operations  14.2 us (6%)
  blocking collectives  12.1 us (6%)
  local copies, waits for them, and re-layouts  9.35 us (4%)
    all_gather x1, waiting for transfers between devices, on_device(): column = lax.all_gather(owned, REPLICA, axis=0, tiled=True)  98.7 us
    reduce_scatter x1, waiting for transfers between devices, on_device(): lax.psum_scatter(slot_grad, 'replica_1', scatter_dimension=0, tiled=True)  30.8 us
    all_to_all x1, blocking collectives, on_device(): lax.all_to_all(send.reshape(owners, capacity, 2 * model_width), 'expert',...  12.1 us
    all_to_all x1, starting transfers between devices, on_device(): lax.all_to_all(summed_z.reshape(rows_y * owners, capacity, model_width),...  7.6 us
    all_to_all x1, starting transfers between devices, on_device(): lax.all_to_all(jnp.sum(tiles, axis=0).reshape(owners, capacity), 'expert'...  6.52 us
    all_to_all x1, starting transfers between devices, on_device(): lax.all_to_all(partial_value.reshape(rows_y * rows_z, slot_count), REPLIC...  5.36 us
    all_to_all x1, waiting for transfers between devices, on_device(): lax.all_to_all(summed_z.reshape(rows_y * owners, capacity, model_width),...  4.81 us
    dot_general x1, matrix products, on_device(): lax.dot_general(up_pre_grad, gathered, leading, preferred_element_type=jn...  4.57 us
  transfers between devices with their start and end apart: 5, of which 3 were waited for; matrix products, arithmetic and copies ran while one was open for 8% of the time, Pallas kernels for 0%

profile of v1, /device:TPU:1, one launch (start us, length us, event | category | flops | bytes accessed | tf_op | source)
XLA Modules:
  0.0 218.2 jit_solution(10834757476153381897)
XLA Ops:
  7.2 0.9 copy.31
  8.5 0.8 copy.33
  9.4 1.1 fusion
  10.8 12.1 %all_to_all.28 = bf16[8,2,8192]{2,1,0:T(2,128)(2,1)S(1)} all-to-all(bf16[8,2,8192]{2,1,0:T(2,128)(2,1)S(1)} %reshape.66), channel_id=1, replica_groups=mesh['expert'=8,'replica_0'=4,'replica_1'=8] {'expert'}, dimensions={0} | all-to-all | bytes 524288 | tf_op jit(solution)/shard_map/all_to_all | solution.py:52
  22.9 0.8 reshape.67
  23.7 98.7 %all-gather.2.cloned.1.call-done = bf16[512,8192]{1,0:T(8,128)(2,1)} async-done(((bf16[16,8192]{1,0:T(8,128)(2,1)}), bf16[512,8192]{1,0:T(8,128)(2,1)}) %all-gather.2.cloned.1.call-update) | async-done | bytes 8388624 | tf_op jit(solution)/shard_map/all_gather | solution.py:55
  122.4 4.3 %fusion.9 = f32[512,224]{0,1:T(8,128)S(1)} fusion(bf16[512,8192]{1,0:T(8,128)(2,1)} %all-gather.2.cloned.1.call-done, bf16[1,224,4096]{2,1,0:T(8,128)(2,1)} %param.12), kind=kOutput, calls=%fused_computation.15 | convolution fusion | flops 939524096 | bytes 6488064 | tf_op jit(solution)/shard_map/dot_general | solution.py:59
  126.8 0.8 copy-done.2
  127.6 1.4 fusion.11
  129.1 1.6 multiply_reduce_fusion
  131.0 1.3 fusion.16
  132.5 3.2 %add_convert_fusion = bf16[512,4096]{1,0:T(8,128)(2,1)} fusion(f32[512,4096]{1,0:T(8,128)S(1)} %fusion.16, bf16[512,224]{1,0:T(8,128)(2,1)S(1)} %bitcast.38, bf16[1,224,4096]{2,1,0:T(8,128)(2,1)S(1)} %copy-done.1), kind=kOutput, calls=%fused_computation.2 | convolution fusion | flops 943718400 | bytes 14647296 | tf_op jit(solution)/shard_map/dot_general | solution.py:76
  135.8 0.7 all_to_all.19
  136.5 5.4 %all-to-all-start.1 = ((f32[32,1,16]{2,1,0:T(1,128)}), f32[32,1,16]{2,1,0:T(1,128)S(1)}, u32[]{:S(2)}, u32[]{:S(2)}) async-start(f32[32,1,16]{2,1,0:T(1,128)} %bitcast.3), calls=%async_computation.1 | async-start | bytes 32768 | tf_op jit(solution)/shard_map/all_to_all | solution.py:79
  141.9 4.6 %fusion.2 = bf16[1,224,4096]{2,1,0:T(8,128)(2,1)} fusion(bf16[512,224]{0,1:T(8,128)(2,1)S(1)} %get-tuple-element.15, bf16[512,8192]{1,0:T(8,128)(2,1)} %all-gather.2.cloned.1.call-done), kind=kOutput, calls=%fused_computation.7 | convolution fusion | flops 940441600 | bytes 6258688 | tf_op jit(solution)/shard_map/dot_general | solution.py:93
  146.4 4.6 %fusion.1 = bf16[1,224,4096]{2,1,0:T(8,128)(2,1)} fusion(bf16[512,224]{0,1:T(8,128)(2,1)S(1)} %get-tuple-element.14, bf16[512,8192]{1,0:T(8,128)(2,1)} %all-gather.2.cloned.1.call-done), kind=kOutput, calls=%fused_computation.6 | convolution fusion | flops 940441600 | bytes 6258688 | tf_op jit(solution)/shard_map/dot_general | solution.py:90
  151.1 0.7 all_to_all.21
  151.7 6.5 %all-to-all-start.2 = ((f32[8,1,2]{2,1,0:T(1,128)}), f32[8,1,2]{2,1,0:T(1,128)S(1)}, u32[]{:S(2)}, u32[]{:S(2)}) async-start(f32[8,1,2]{2,1,0:T(1,128)} %bitcast.4), calls=%async_computation.2 | async-start | bytes 8192 | tf_op jit(solution)/shard_map/all_to_all | solution.py:82
  158.2 30.8 %reduce-scatter.2.cloned.1.call-done = bf16[64,4096]{1,0:T(8,128)(2,1)} async-done(((bf16[512,4096]{1,0:T(8,128)(2,1)}), bf16[64,4096]{1,0:T(8,128)(2,1)}) %reduce-scatter.2.cloned.1.call-update) | async-done | bytes 524304 | tf_op jit(solution)/shard_map/reduce_scatter | solution.py:78
  189.0 2.2 %reshape.72 = bf16[32,2,4096]{2,1,0:T(2,128)(2,1)} reshape(bf16[64,4096]{1,0:T(8,128)(2,1)} %reduce-scatter.2.cloned.1.call-done) | data formatting | bytes 1048576 | tf_op jit(solution)/shard_map/reshape | solution.py:97
  191.3 7.6 %all-to-all-start.3 = ((bf16[32,2,4096]{2,1,0:T(2,128)(2,1)}), bf16[32,2,4096]{2,1,0:T(2,128)(2,1)S(1)}, u32[]{:S(2)}, u32[]{:S(2)}) async-start(bf16[32,2,4096]{2,1,0:T(2,128)(2,1)} %reshape.72), calls=%async_computation.4 | async-start | bytes 1048576 | tf_op jit(solution)/shard_map/all_to_all | solution.py:96
  198.9 4.5 %fusion.3 = bf16[1,224,4096]{2,1,0:T(8,128)(2,1)} fusion(bf16[512,224]{0,1:T(8,128)(2,1)S(1)} %get-tuple-element.13, bf16[512,8192]{1,0:T(8,128)(2,1)} %all-gather.2.cloned.1.call-done), kind=kOutput, calls=%fused_computation.8 | convolution fusion | flops 940441600 | bytes 6258688 | tf_op jit(solution)/shard_map/dot_general | solution.py:87
  205.5 4.8 %all-to-all-done.3 = bf16[32,2,4096]{2,1,0:T(2,128)(2,1)S(1)} async-done(((bf16[32,2,4096]{2,1,0:T(2,128)(2,1)}), bf16[32,2,4096]{2,1,0:T(2,128)(2,1)S(1)}, u32[]{:S(2)}, u32[]{:S(2)}) %all-to-all-start.3) | async-done | bytes 524320 | tf_op jit(solution)/shard_map/all_to_all | solution.py:96
  210.5 0.9 convolution_convert_fusion.3
  (32 shorter events, 3.8 us)
Async XLA Ops:
  7.2 119.6 %copy-start = (bf16[1,224,4096]{2,1,0:T(8,128)(2,1)S(1)}, bf16[1,224,4096]{2,1,0:T(8,128)(2,1)}, u32[]{:S(2)}) copy-start(bf16[1,224,4096]{2,1,0:T(8,128)(2,1)} %param.11) | copy-start | bytes 5505028
  7.2 115.3 %all-gather.2.cloned.1.call-start = ((), (), s32[]{:S(2)}) async-start(), calls=%async_computation.5 | async-start | bytes 8650752 | tf_op jit(solution)/shard_map/all_gather | solution.py:55
  23.7 165.4 %reduce-scatter.2.cloned.1.call-start = ((), (), s32[]{:S(2)}) async-start(), calls=%async_computation.6 | async-start | bytes 4718592 | tf_op jit(solution)/shard_map/reduce_scatter | solution.py:78
  122.4 5.2 %copy-start.2 = (bf16[512,8192]{1,0:T(8,128)(2,1)S(1)}, bf16[512,8192]{1,0:T(8,128)(2,1)}, u32[]{:S(2)}) copy-start(bf16[512,8192]{1,0:T(8,128)(2,1)} %all-gather.2.cloned.1.call-done) | copy-start | bytes 25165828
  127.6 1.5 copy-start.3
  131.0 1.5 copy-start.1
  136.5 14.5 %all-to-all-start.1 = ((f32[32,1,16]{2,1,0:T(1,128)}), f32[32,1,16]{2,1,0:T(1,128)S(1)}, u32[]{:S(2)}, u32[]{:S(2)}) async-start(f32[32,1,16]{2,1,0:T(1,128)} %bitcast.3), calls=%async_computation.1 | async-start | bytes 32768 | tf_op jit(solution)/shard_map/all_to_all | solution.py:79
  151.7 39.5 %all-to-all-start.2 = ((f32[8,1,2]{2,1,0:T(1,128)}), f32[8,1,2]{2,1,0:T(1,128)S(1)}, u32[]{:S(2)}, u32[]{:S(2)}) async-start(f32[8,1,2]{2,1,0:T(1,128)} %bitcast.4), calls=%async_computation.2 | async-start | bytes 8192 | tf_op jit(solution)/shard_map/all_to_all | solution.py:82
  191.3 19.0 %all-to-all-start.3 = ((bf16[32,2,4096]{2,1,0:T(2,128)(2,1)}), bf16[32,2,4096]{2,1,0:T(2,128)(2,1)S(1)}, u32[]{:S(2)}, u32[]{:S(2)}) async-start(bf16[32,2,4096]{2,1,0:T(2,128)(2,1)} %reshape.72), calls=%async_computation.4 | async-start | bytes 1048576 | tf_op jit(solution)/shard_map/all_to_all | solution.py:96
Sparse Core Ops, SparseCore 0:
  23.8 98.5 all-gather.1
  135.9 53.0 reduce-scatter.1
